TPU v7x, 32 devices: a whole 2x2x4 slice. The times are simulated.
32 devices in a mesh: tile: 8 (over z, x), pos: 4 (over y, core).
Axes of the slice: x: 2, y: 2, z: 4, core: 2. Of those that a mesh axis runs over, the one named last changes fastest.
Arguments:
- object_tiles: bfloat16 [8, 2, 512, 512], P('tile', None, 'pos'), may hold values from -4.1875 to 4.1875
- probe: float32 [2, 256, 256], replicated, may hold values from -4.2 to 4.2
- frames: bfloat16 [512, 256, 256], P(('tile', 'pos')), may hold values from 0 to 60, as said below
- offsets: int32 [2, 512], P(None, ('tile', 'pos')), may hold values from 1 to 511
Outputs:
- shifts: float32 [2, 512], P(None, ('tile', 'pos'))
- losses: float32 [512], P(('tile', 'pos'))
Inputs may be any that keep to these rules, and one draw needn't show every extreme that they name: `frames`: amplitudes are not negative.
All inputs are finite; a program needn't handle non-finite values.
Results may differ from a plain program's by a relative error of at most 0.0097.
Values may be sent and summed in bfloat16 or wider, within the bound.
A program may use at most 128 MiB of HBM per device.

v0:
```python
import math

import jax
import jax.numpy as jnp
from jax import lax
from jax.sharding import PartitionSpec as P

PROBE = 256
GC = 4


def passed_along(x, axis, by):
    devices = lax.axis_size(axis)
    pairs = [(i, i + by) for i in range(devices) if 0 <= i + by < devices]
    return lax.ppermute(x, axis, pairs)


def dft_tables(length_n):
    indices = jnp.arange(length_n, dtype=jnp.int32)
    products_mod = indices[:, None] * indices[None, :] % length_n
    angles = products_mod.astype(jnp.float32) * (2.0 * math.pi / length_n)
    factor = 1.0 / math.sqrt(length_n)
    return (
        (jnp.cos(angles) * factor).astype(jnp.bfloat16),
        (jnp.sin(angles) * factor).astype(jnp.bfloat16),
    )


def left_apply(table, stacked):
    return jnp.einsum("kn,pnm->pkm", table, stacked, preferred_element_type=jnp.float32)


def right_apply(stacked, table):
    return jnp.einsum("pkn,nm->pkm", stacked, table, preferred_element_type=jnp.float32)


def refine_block(windows, probe, detectors, cosine_table, sine_table):
    length_n = detectors.shape[1]
    window_f = windows.astype(jnp.float32)
    patch = window_f[:, :, 1:-1, 1:-1]
    along_row = 0.5 * (window_f[:, :, 2:, 1:-1] - window_f[:, :, :-2, 1:-1])
    along_col = 0.5 * (window_f[:, :, 1:-1, 2:] - window_f[:, :, 1:-1, :-2])
    exit_re = probe[0] * patch[:, 0] - probe[1] * patch[:, 1]
    exit_im = probe[0] * patch[:, 1] + probe[1] * patch[:, 0]
    stacked = jnp.concatenate([exit_re, exit_im], axis=2).astype(jnp.bfloat16)
    by_cosine = left_apply(cosine_table, stacked)
    by_sine = left_apply(sine_table, stacked)
    half_re = by_cosine[:, :, :length_n] + by_sine[:, :, length_n:]
    half_im = by_cosine[:, :, length_n:] - by_sine[:, :, :length_n]
    row_pairs = jnp.concatenate([half_re, half_im], axis=1).astype(jnp.bfloat16)
    rows_cosine = right_apply(row_pairs, cosine_table)
    rows_sine = right_apply(row_pairs, sine_table)
    far_re = rows_cosine[:, :length_n] + rows_sine[:, length_n:]
    far_im = rows_cosine[:, length_n:] - rows_sine[:, :length_n]
    magnitude = jnp.sqrt(far_re * far_re + far_im * far_im)
    keep_part = 1.0 - detectors.astype(jnp.float32) / jnp.maximum(magnitude, 0.25)
    resid_re = far_re * keep_part
    resid_im = far_im * keep_part
    losses = jnp.mean(resid_re * resid_re + resid_im * resid_im, axis=(1, 2))
    stacked_back = jnp.concatenate([resid_re, resid_im], axis=2).astype(jnp.bfloat16)
    back_cosine = left_apply(cosine_table, stacked_back)
    back_sine = left_apply(sine_table, stacked_back)
    inner_re = back_cosine[:, :, :length_n] - back_sine[:, :, length_n:]
    inner_im = back_cosine[:, :, length_n:] + back_sine[:, :, :length_n]
    inner_pairs = jnp.concatenate([inner_re, inner_im], axis=1).astype(jnp.bfloat16)
    final_cosine = right_apply(inner_pairs, cosine_table)
    final_sine = right_apply(inner_pairs, sine_table)
    wave_re = final_cosine[:, :length_n] - final_sine[:, length_n:]
    wave_im = final_cosine[:, length_n:] + final_sine[:, :length_n]

    def slope_of(derived):
        probed_re = probe[0] * derived[:, 0] - probe[1] * derived[:, 1]
        probed_im = probe[0] * derived[:, 1] + probe[1] * derived[:, 0]
        return jnp.sum(wave_re * probed_re + wave_im * probed_im, axis=(1, 2))

    return (jnp.stack([slope_of(along_row), slope_of(along_col)], axis=1), losses)


def fetch_side(block, offset_by, inside):
    arrived = passed_along(block, "tile", offset_by)
    return jnp.where(inside, arrived, jnp.zeros_like(arrived))


def fetch_rim(block, offset_by):
    return passed_along(block, "tile", offset_by)


def local(object_tiles, probe, frames, offsets):
    quarter = object_tiles[0]
    region_col = lax.axis_index("tile") % GC
    margin = PROBE // 2
    region_block = lax.all_gather(quarter, "pos", axis=1, tiled=True)
    west_strip = fetch_side(region_block[:, :, -margin:], 1, region_col > 0)
    east_strip = fetch_side(region_block[:, :, :margin], -1, region_col < GC - 1)
    middle = jnp.concatenate([west_strip, region_block, east_strip], axis=2)
    north_strip = fetch_rim(middle[:, -margin:, :], GC)
    south_strip = fetch_rim(middle[:, :margin, :], -GC)
    padded = jnp.concatenate([north_strip, middle, south_strip], axis=1)
    cosine_table, sine_table = dft_tables(PROBE)

    def window_at(start_row, start_col):
        return lax.dynamic_slice(
            padded,
            (jnp.zeros((), jnp.int32), start_row - 1, start_col - 1),
            (2, PROBE + 2, PROBE + 2),
        )

    windows = jax.vmap(window_at)(offsets[0], offsets[1])
    slopes, losses = refine_block(windows, probe, frames, cosine_table, sine_table)
    total_sq = lax.psum(jnp.sum(slopes * slopes), ("tile", "pos"))
    positions_all = frames.shape[0] * lax.axis_size("tile") * lax.axis_size("pos")
    norm_scale = jnp.sqrt(total_sq / positions_all + 1e-06)
    return ((-slopes / norm_scale).T, losses)


def solution(mesh):
    in_specs = (
        P("tile", None, "pos", None),
        P(),
        P(("tile", "pos"), None, None),
        P(None, ("tile", "pos")),
    )
    out_specs = (P(None, ("tile", "pos")), P(("tile", "pos")))
    return jax.shard_map(local, mesh=mesh, in_specs=in_specs, out_specs=out_specs, check_vma=False)
```

profile of v0, /device:TPU:0, one launch (start us, length us, event | category | flops | bytes accessed | tf_op | source)
XLA Modules:
  0.0 224.4 jit_solution(8021981490494316017)
XLA Ops:
  7.2 0.7 all-gather.3.cloned.1.call-update
  7.9 21.1 %all-gather.3.cloned.1.call-done = bf16[1,2,512,512]{3,2,1,0:T(8,128)(2,1)} async-done(((bf16[1,2,128,512]{3,2,1,0:T(8,128)(2,1)}), bf16[1,2,512,512]{3,2,1,0:T(8,128)(2,1)}) %all-gather.3.cloned.1.call-update) | async-done | bytes 1048592 | tf_op jit(solution)/shard_map/all_gather | solution.py:92
  29.0 1.8 fusion.79
  30.8 1.3 collective-permute-start.1
  32.1 4.6 %collective-permute-start = (bf16[2,512,128]{2,1,0:T(8,128)(2,1)}, bf16[2,512,128]{2,1,0:T(8,128)(2,1)S(1)}, u32[]{:S(2)}, u32[]{:S(2)}) collective-permute-start(bf16[2,512,128]{2,1,0:T(8,128)(2,1)} %get-tuple-element.35), channel_id=1, source_target_pairs={{0,4},{4,8},{8,12},{12,16},{16,20},{20,24},{24,28},{1,5},{5,9},{9,... | collective-permute-start | bytes 786440 | tf_op jit(solution)/shard_map/ppermute | solution.py:15
  36.7 4.4 %collective-permute-done.1 = bf16[2,512,128]{2,1,0:T(8,128)(2,1)S(1)} collective-permute-done((bf16[2,512,128]{2,1,0:T(8,128)(2,1)S(1)}, bf16[2,512,128]{2,1,0:T(8,128)(2,1)S(1)}, u32[]{:S(2)}, u32[]{:S(2)}) %collective-permute-start.1) | collective-permute-done | bytes 262176 | tf_op jit(solution)/shard_map/ppermute | solution.py:15
  41.1 5.6 %collective-permute-done = bf16[2,512,128]{2,1,0:T(8,128)(2,1)S(1)} collective-permute-done((bf16[2,512,128]{2,1,0:T(8,128)(2,1)}, bf16[2,512,128]{2,1,0:T(8,128)(2,1)S(1)}, u32[]{:S(2)}, u32[]{:S(2)}) %collective-permute-start) | collective-permute-done | bytes 262176 | tf_op jit(solution)/shard_map/ppermute | solution.py:15
  46.8 2.2 pad_maximum_fusion.15
  48.9 1.3 collective-permute-start.3
  50.2 7.0 %collective-permute-start.2 = (bf16[2,128,768]{2,1,0:T(8,128)(2,1)}, bf16[2,128,768]{2,1,0:T(8,128)(2,1)}, u32[]{:S(2)}, u32[]{:S(2)}) collective-permute-start(bf16[2,128,768]{2,1,0:T(8,128)(2,1)} %get-tuple-element.33), channel_id=1, source_target_pairs={{0,16},{4,20},{8,24},{12,28},{1,17},{5,21},{9,25},{13,29},{2,18},{... | collective-permute-start | bytes 1179656 | tf_op jit(solution)/shard_map/ppermute | solution.py:15
  57.2 2.4 %copy.9 = bf16[16,256,256]{1,2,0:T(8,128)(2,1)} copy(bf16[16,256,256]{2,1,0:T(8,128)(2,1)S(1)} %copy-done.7) | data formatting | bytes 4194304 | tf_op args[2]
  59.6 1.9 slice_bitcast_fusion.7
  61.5 10.0 %collective-permute-done.3 = bf16[2,128,768]{2,1,0:T(8,128)(2,1)} collective-permute-done((bf16[2,128,768]{2,1,0:T(8,128)(2,1)}, bf16[2,128,768]{2,1,0:T(8,128)(2,1)}, u32[]{:S(2)}, u32[]{:S(2)}) %collective-permute-start.3) | collective-permute-done | bytes 393248 | tf_op jit(solution)/shard_map/ppermute | solution.py:15
  71.5 1.5 pad_maximum_fusion.12
  73.0 46.8 %while.1 = (s32[]{:T(128)}, bf16[2,768,768]{2,1,0:T(8,128)(2,1)S(1)}, s32[16,3]{0,1:T(4,128)S(1)}, bf16[16,2,258,258]{3,2,0,1:T(8,128)(2,1)}, s32[]{:T(128)}) while((s32[]{:T(128)}, bf16[2,768,768]{2,1,0:T(8,128)(2,1)S(1)}, s32[16,3]{0,1:T(4,128)S(1)}, bf16[16,2,258,258]{3,2,0,1:T(8,128)(2,1)}, s32[]{:T(128)}) %tuple.35), condition=%wide.while_cond, body=%wide.while_body.sunk | while | flops 2 | bytes 672901 | solution.py:102
  73.7 2.3 %bitcast_dynamic-update-slice_fusion.2 = bf16[16,2,258,258]{3,2,0,1:T(8,128)(2,1)} fusion(bf16[16,2,258,258]{3,2,0,1:T(8,128)(2,1)} %get-tuple-element.81, s32[]{:T(128)S(6)} %copy.23, bf16[2,768,768]{2,1,0:T(8,128)(2,1)S(1)} %get-tuple-element.84, s32[]{:T(128)} %bitcast.77, s32[]{:T(128)} %bitcast.78), kind=kLoop, calls=%fused_computation.clone.1 | loop fusion | bytes 672788 | tf_op jit(solution)/shard_map/vmap()/gather
  76.6 2.3 %bitcast_dynamic-update-slice_fusion.2 = bf16[16,2,258,258]{3,2,0,1:T(8,128)(2,1)} fusion(bf16[16,2,258,258]{3,2,0,1:T(8,128)(2,1)} %get-tuple-element.81, s32[]{:T(128)S(6)} %copy.23, bf16[2,768,768]{2,1,0:T(8,128)(2,1)S(1)} %get-tuple-element.84, s32[]{:T(128)} %bitcast.77, s32[]{:T(128)} %bitcast.78), kind=kLoop, calls=%fused_computation.clone.1 | loop fusion | bytes 672788 | tf_op jit(solution)/shard_map/vmap()/gather
  79.5 2.3 %bitcast_dynamic-update-slice_fusion.2 = bf16[16,2,258,258]{3,2,0,1:T(8,128)(2,1)} fusion(bf16[16,2,258,258]{3,2,0,1:T(8,128)(2,1)} %get-tuple-element.81, s32[]{:T(128)S(6)} %copy.23, bf16[2,768,768]{2,1,0:T(8,128)(2,1)S(1)} %get-tuple-element.84, s32[]{:T(128)} %bitcast.77, s32[]{:T(128)} %bitcast.78), kind=kLoop, calls=%fused_computation.clone.1 | loop fusion | bytes 672788 | tf_op jit(solution)/shard_map/vmap()/gather
  82.4 2.3 %bitcast_dynamic-update-slice_fusion.2 = bf16[16,2,258,258]{3,2,0,1:T(8,128)(2,1)} fusion(bf16[16,2,258,258]{3,2,0,1:T(8,128)(2,1)} %get-tuple-element.81, s32[]{:T(128)S(6)} %copy.23, bf16[2,768,768]{2,1,0:T(8,128)(2,1)S(1)} %get-tuple-element.84, s32[]{:T(128)} %bitcast.77, s32[]{:T(128)} %bitcast.78), kind=kLoop, calls=%fused_computation.clone.1 | loop fusion | bytes 672788 | tf_op jit(solution)/shard_map/vmap()/gather
  85.3 2.3 %bitcast_dynamic-update-slice_fusion.2 = bf16[16,2,258,258]{3,2,0,1:T(8,128)(2,1)} fusion(bf16[16,2,258,258]{3,2,0,1:T(8,128)(2,1)} %get-tuple-element.81, s32[]{:T(128)S(6)} %copy.23, bf16[2,768,768]{2,1,0:T(8,128)(2,1)S(1)} %get-tuple-element.84, s32[]{:T(128)} %bitcast.77, s32[]{:T(128)} %bitcast.78), kind=kLoop, calls=%fused_computation.clone.1 | loop fusion | bytes 672788 | tf_op jit(solution)/shard_map/vmap()/gather
  88.2 2.3 %bitcast_dynamic-update-slice_fusion.2 = bf16[16,2,258,258]{3,2,0,1:T(8,128)(2,1)} fusion(bf16[16,2,258,258]{3,2,0,1:T(8,128)(2,1)} %get-tuple-element.81, s32[]{:T(128)S(6)} %copy.23, bf16[2,768,768]{2,1,0:T(8,128)(2,1)S(1)} %get-tuple-element.84, s32[]{:T(128)} %bitcast.77, s32[]{:T(128)} %bitcast.78), kind=kLoop, calls=%fused_computation.clone.1 | loop fusion | bytes 672788 | tf_op jit(solution)/shard_map/vmap()/gather
  91.2 2.3 %bitcast_dynamic-update-slice_fusion.2 = bf16[16,2,258,258]{3,2,0,1:T(8,128)(2,1)} fusion(bf16[16,2,258,258]{3,2,0,1:T(8,128)(2,1)} %get-tuple-element.81, s32[]{:T(128)S(6)} %copy.23, bf16[2,768,768]{2,1,0:T(8,128)(2,1)S(1)} %get-tuple-element.84, s32[]{:T(128)} %bitcast.77, s32[]{:T(128)} %bitcast.78), kind=kLoop, calls=%fused_computation.clone.1 | loop fusion | bytes 672788 | tf_op jit(solution)/shard_map/vmap()/gather
  94.1 2.3 %bitcast_dynamic-update-slice_fusion.2 = bf16[16,2,258,258]{3,2,0,1:T(8,128)(2,1)} fusion(bf16[16,2,258,258]{3,2,0,1:T(8,128)(2,1)} %get-tuple-element.81, s32[]{:T(128)S(6)} %copy.23, bf16[2,768,768]{2,1,0:T(8,128)(2,1)S(1)} %get-tuple-element.84, s32[]{:T(128)} %bitcast.77, s32[]{:T(128)} %bitcast.78), kind=kLoop, calls=%fused_computation.clone.1 | loop fusion | bytes 672788 | tf_op jit(solution)/shard_map/vmap()/gather
  97.0 2.3 %bitcast_dynamic-update-slice_fusion.2 = bf16[16,2,258,258]{3,2,0,1:T(8,128)(2,1)} fusion(bf16[16,2,258,258]{3,2,0,1:T(8,128)(2,1)} %get-tuple-element.81, s32[]{:T(128)S(6)} %copy.23, bf16[2,768,768]{2,1,0:T(8,128)(2,1)S(1)} %get-tuple-element.84, s32[]{:T(128)} %bitcast.77, s32[]{:T(128)} %bitcast.78), kind=kLoop, calls=%fused_computation.clone.1 | loop fusion | bytes 672788 | tf_op jit(solution)/shard_map/vmap()/gather
  100.0 2.3 %bitcast_dynamic-update-slice_fusion.2 = bf16[16,2,258,258]{3,2,0,1:T(8,128)(2,1)} fusion(bf16[16,2,258,258]{3,2,0,1:T(8,128)(2,1)} %get-tuple-element.81, s32[]{:T(128)S(6)} %copy.23, bf16[2,768,768]{2,1,0:T(8,128)(2,1)S(1)} %get-tuple-element.84, s32[]{:T(128)} %bitcast.77, s32[]{:T(128)} %bitcast.78), kind=kLoop, calls=%fused_computation.clone.1 | loop fusion | bytes 672788 | tf_op jit(solution)/shard_map/vmap()/gather
  102.9 2.3 %bitcast_dynamic-update-slice_fusion.2 = bf16[16,2,258,258]{3,2,0,1:T(8,128)(2,1)} fusion(bf16[16,2,258,258]{3,2,0,1:T(8,128)(2,1)} %get-tuple-element.81, s32[]{:T(128)S(6)} %copy.23, bf16[2,768,768]{2,1,0:T(8,128)(2,1)S(1)} %get-tuple-element.84, s32[]{:T(128)} %bitcast.77, s32[]{:T(128)} %bitcast.78), kind=kLoop, calls=%fused_computation.clone.1 | loop fusion | bytes 672788 | tf_op jit(solution)/shard_map/vmap()/gather
  105.8 2.3 %bitcast_dynamic-update-slice_fusion.2 = bf16[16,2,258,258]{3,2,0,1:T(8,128)(2,1)} fusion(bf16[16,2,258,258]{3,2,0,1:T(8,128)(2,1)} %get-tuple-element.81, s32[]{:T(128)S(6)} %copy.23, bf16[2,768,768]{2,1,0:T(8,128)(2,1)S(1)} %get-tuple-element.84, s32[]{:T(128)} %bitcast.77, s32[]{:T(128)} %bitcast.78), kind=kLoop, calls=%fused_computation.clone.1 | loop fusion | bytes 672788 | tf_op jit(solution)/shard_map/vmap()/gather
  108.7 2.3 %bitcast_dynamic-update-slice_fusion.2 = bf16[16,2,258,258]{3,2,0,1:T(8,128)(2,1)} fusion(bf16[16,2,258,258]{3,2,0,1:T(8,128)(2,1)} %get-tuple-element.81, s32[]{:T(128)S(6)} %copy.23, bf16[2,768,768]{2,1,0:T(8,128)(2,1)S(1)} %get-tuple-element.84, s32[]{:T(128)} %bitcast.77, s32[]{:T(128)} %bitcast.78), kind=kLoop, calls=%fused_computation.clone.1 | loop fusion | bytes 672788 | tf_op jit(solution)/shard_map/vmap()/gather
  111.7 2.3 %bitcast_dynamic-update-slice_fusion.2 = bf16[16,2,258,258]{3,2,0,1:T(8,128)(2,1)} fusion(bf16[16,2,258,258]{3,2,0,1:T(8,128)(2,1)} %get-tuple-element.81, s32[]{:T(128)S(6)} %copy.23, bf16[2,768,768]{2,1,0:T(8,128)(2,1)S(1)} %get-tuple-element.84, s32[]{:T(128)} %bitcast.77, s32[]{:T(128)} %bitcast.78), kind=kLoop, calls=%fused_computation.clone.1 | loop fusion | bytes 672788 | tf_op jit(solution)/shard_map/vmap()/gather
  114.6 2.3 %bitcast_dynamic-update-slice_fusion.2 = bf16[16,2,258,258]{3,2,0,1:T(8,128)(2,1)} fusion(bf16[16,2,258,258]{3,2,0,1:T(8,128)(2,1)} %get-tuple-element.81, s32[]{:T(128)S(6)} %copy.23, bf16[2,768,768]{2,1,0:T(8,128)(2,1)S(1)} %get-tuple-element.84, s32[]{:T(128)} %bitcast.77, s32[]{:T(128)} %bitcast.78), kind=kLoop, calls=%fused_computation.clone.1 | loop fusion | bytes 672788 | tf_op jit(solution)/shard_map/vmap()/gather
  117.5 2.3 %bitcast_dynamic-update-slice_fusion.2 = bf16[16,2,258,258]{3,2,0,1:T(8,128)(2,1)} fusion(bf16[16,2,258,258]{3,2,0,1:T(8,128)(2,1)} %get-tuple-element.81, s32[]{:T(128)S(6)} %copy.23, bf16[2,768,768]{2,1,0:T(8,128)(2,1)S(1)} %get-tuple-element.84, s32[]{:T(128)} %bitcast.77, s32[]{:T(128)} %bitcast.78), kind=kLoop, calls=%fused_computation.clone.1 | loop fusion | bytes 672788 | tf_op jit(solution)/shard_map/vmap()/gather
  119.8 3.7 %convert_element_type.45 = f32[16,2,258,258]{3,2,0,1:T(8,128)S(1)} convert(bf16[16,2,258,258]{3,2,0,1:T(8,128)(2,1)} %get-tuple-element.9) | non-fusion elementwise | flops 2130048 | bytes 12780288 | tf_op jit(solution)/shard_map/convert_element_type | solution.py:39
  123.5 9.2 %fusion = (f32[16,2,256,256]{3,2,0,1:T(8,128)}, f32[16,2,256,256]{3,2,0,1:T(8,128)}) fusion(f32[16,2,258,258]{3,2,0,1:T(8,128)S(1)} %convert_element_type.45), kind=kLoop, calls=%fused_computation.3 | loop fusion | flops 8388608 | bytes 50331648 | tf_op jit(solution)/shard_map/mul | solution.py:42
  132.7 4.7 %subtract_convert_fusion = (bf16[16,256,256]{2,1,0:T(8,128)(2,1)S(1)}, bf16[16,256,256]{2,1,0:T(8,128)(2,1)}) fusion(f32[16,2,258,258]{3,2,0,1:T(8,128)S(1)} %convert_element_type.45, f32[256,256]{1,0:T(8,128)S(1)} %copy-done.4, f32[256,256]{1,0:T(8,128)S(1)} %copy-done.3), kind=kLoop, calls=%fused_computation.35 | loop fusion | flops 8388608 | bytes 13107200 | tf_op jit(solution)/shard_map/convert.6
  137.4 3.9 %convolution_bitcast_fusion = f32[16,256,512]{2,1,0:T(8,128)S(1)} fusion(bf16[16,256,256]{2,1,0:T(8,128)(2,1)} %get-tuple-element.30, bf16[16,256,256]{2,1,0:T(8,128)(2,1)S(1)} %get-tuple-element.29), kind=kOutput, calls=%fused_computation.36 | convolution fusion | flops 1083179008 | bytes 12582912 | tf_op jit(solution)/shard_map/kn,pnm->pkm/dot_general | solution.py:30
  141.3 2.2 convolution_bitcast_fusion.1
  143.5 1.9 fusion.5
  145.4 2.2 fusion.10
  147.6 2.3 %fusion.11 = f32[16,512,256]{1,2,0:T(8,128)S(1)} fusion(bf16[16,256,256]{2,1,0:T(8,128)(2,1)S(1)} %get-tuple-element.28, bf16[16,256,256]{2,1,0:T(8,128)(2,1)S(1)} %get-tuple-element.27), kind=kOutput, calls=%fused_computation.43 | convolution fusion | flops 1083179008 | bytes 12582912 | tf_op jit(solution)/shard_map/pkn,nm->pkm/dot_general | solution.py:34
  149.9 3.8 %add_reduce_fusion = (f32[16]{0:T(128)S(1)}, bf16[16,256,256]{1,2,0:T(8,128)(2,1)S(1)}, bf16[16,256,256]{1,2,0:T(8,128)(2,1)S(1)}) fusion(f32[16,512,256]{1,2,0:T(8,128)S(1)} %fusion.10, f32[16,512,256]{1,2,0:T(8,128)S(1)} %fusion.11, bf16[16,256,256]{1,2,0:T(8,128)(2,1)S(1)} %copy-done.1), kind=kLoop, calls=%fused_computation.28 | loop fusion | flops 17825776 | bytes 23068736 | tf_op jit(solution)/shard_map/reduce_sum | solution.py:59
  153.7 2.2 convolution_bitcast_fusion.2
  155.9 2.2 convolution_bitcast_fusion.3
  158.1 1.9 fusion.3
  160.0 2.2 fusion.8
  162.2 2.2 fusion.9
  164.4 8.2 %add_reduce_fusion.2 = (f32[16]{0:T(128)S(1)}, f32[16]{0:T(128)S(1)}) fusion(f32[16,2,256,256]{3,2,0,1:T(8,128)} %get-tuple-element.32, f32[256,256]{1,0:T(8,128)S(1)} %copy-done.4, f32[256,256]{1,0:T(8,128)S(1)} %copy-done.3, f32[16,512,256]{2,1,0:T(8,128)S(1)} %fusion.8, f32[16,512,256]{2,1,0:T(8,128)S(1)} %fusion.9, f32[16,2,256,256]{3,2,0,1:T(8,128)} %get-tuple-element.31), kind=kLoop, calls=%fused_computation.30 | loop fusion | flops 23068640 | bytes 34078848 | tf_op jit(solution)/shard_map/reduce_sum | solution.py:74
  172.6 0.6 multiply_reduce_fusion
  173.2 42.6 %psum.7 = f32[]{:T(128)} all-reduce(f32[]{:T(128)} %multiply_reduce_fusion), channel_id=1, replica_groups=mesh['tile'=8,'pos'=4] {'tile','pos'}, use_global_device_ids=true, to_apply=%region_3.4 | all-reduce | flops 1 | bytes 8 | tf_op jit(solution)/shard_map/psum | solution.py:110
  (60 shorter events, 11.5 us)
Async XLA Ops:
  7.2 50.0 %copy-start.8 = (s32[2,16]{1,0:T(2,128)S(1)}, s32[2,16]{1,0:T(2,128)}, u32[]{:S(2)}) copy-start(s32[2,16]{1,0:T(2,128)} %param.7) | copy-start | bytes 388
  7.2 50.0 %copy-start.7 = (bf16[16,256,256]{2,1,0:T(8,128)(2,1)S(1)}, bf16[16,256,256]{2,1,0:T(8,128)(2,1)}, u32[]{:S(2)}) copy-start(bf16[16,256,256]{2,1,0:T(8,128)(2,1)} %param.6) | copy-start | bytes 6291460
  7.2 21.8 %all-gather.3.cloned.1.call-start = ((), (), s32[]{:S(2)}) async-start(), calls=%async_computation | async-start | bytes 1310720 | tf_op jit(solution)/shard_map/all_gather | solution.py:92
  30.8 10.3 %collective-permute-start.1 = (bf16[2,512,128]{2,1,0:T(8,128)(2,1)S(1)}, bf16[2,512,128]{2,1,0:T(8,128)(2,1)S(1)}, u32[]{:S(2)}, u32[]{:S(2)}) collective-permute-start(bf16[2,512,128]{2,1,0:T(8,128)(2,1)S(1)} %get-tuple-element.36), channel_id=1, source_target_pairs={{4,0},{8,4},{12,8},{16,12},{20,16},{24,20},{28,24},{5,1},{9,5},{13... | collective-permute-start | bytes 786440 | tf_op jit(solution)/shard_map/ppermute | solution.py:15
  32.1 14.6 %collective-permute-start = (bf16[2,512,128]{2,1,0:T(8,128)(2,1)}, bf16[2,512,128]{2,1,0:T(8,128)(2,1)S(1)}, u32[]{:S(2)}, u32[]{:S(2)}) collective-permute-start(bf16[2,512,128]{2,1,0:T(8,128)(2,1)} %get-tuple-element.35), channel_id=1, source_target_pairs={{0,4},{4,8},{8,12},{12,16},{16,20},{20,24},{24,28},{1,5},{5,9},{9,... | collective-permute-start | bytes 786440 | tf_op jit(solution)/shard_map/ppermute | solution.py:15
  41.1 5.6 %copy-start.5 = (bf16[2,512,128]{2,1,0:T(8,128)(2,1)}, bf16[2,512,128]{2,1,0:T(8,128)(2,1)S(1)}, u32[]{:S(2)}) copy-start(bf16[2,512,128]{2,1,0:T(8,128)(2,1)S(1)} %broadcast_select_fusion) | copy-start | bytes 786436
  41.1 30.3 %copy-start.2 = (bf16[1,2,512,512]{3,2,1,0:T(8,128)(2,1)S(1)}, bf16[1,2,512,512]{3,2,1,0:T(8,128)(2,1)}, u32[]{:S(2)}) copy-start(bf16[1,2,512,512]{3,2,1,0:T(8,128)(2,1)} %all-gather.3.cloned.1.call-done) | copy-start | bytes 3145732
  46.7 2.2 copy-start.6
  48.9 22.6 %collective-permute-start.3 = (bf16[2,128,768]{2,1,0:T(8,128)(2,1)}, bf16[2,128,768]{2,1,0:T(8,128)(2,1)}, u32[]{:S(2)}, u32[]{:S(2)}) collective-permute-start(bf16[2,128,768]{2,1,0:T(8,128)(2,1)} %get-tuple-element.34), channel_id=1, source_target_pairs={{16,0},{20,4},{24,8},{28,12},{17,1},{21,5},{25,9},{29,13},{18,2},{... | collective-permute-start | bytes 1179656 | tf_op jit(solution)/shard_map/ppermute | solution.py:15
  50.2 21.3 %collective-permute-start.2 = (bf16[2,128,768]{2,1,0:T(8,128)(2,1)}, bf16[2,128,768]{2,1,0:T(8,128)(2,1)}, u32[]{:S(2)}, u32[]{:S(2)}) collective-permute-start(bf16[2,128,768]{2,1,0:T(8,128)(2,1)} %get-tuple-element.33), channel_id=1, source_target_pairs={{0,16},{4,20},{8,24},{12,28},{1,17},{5,21},{9,25},{13,29},{2,18},{... | collective-permute-start | bytes 1179656 | tf_op jit(solution)/shard_map/ppermute | solution.py:15
  123.5 9.2 %copy-start.3 = (f32[256,256]{1,0:T(8,128)S(1)}, f32[256,256]{1,0:T(8,128)}, u32[]{:S(2)}) copy-start(f32[256,256]{1,0:T(8,128)} %get-tuple-element.37) | copy-start | bytes 786436
  123.5 9.2 %copy-start.4 = (f32[256,256]{1,0:T(8,128)S(1)}, f32[256,256]{1,0:T(8,128)}, u32[]{:S(2)}) copy-start(f32[256,256]{1,0:T(8,128)} %get-tuple-element.38) | copy-start | bytes 786436
  137.4 3.9 %copy-start = (bf16[16,256,256]{2,1,0:T(8,128)(2,1)S(1)}, bf16[16,256,256]{2,1,0:T(8,128)(2,1)}, u32[]{:S(2)}) copy-start(bf16[16,256,256]{2,1,0:T(8,128)(2,1)} %get-tuple-element.30) | copy-start | bytes 6291460
  147.6 2.3 %copy-start.1 = (bf16[16,256,256]{1,2,0:T(8,128)(2,1)S(1)}, bf16[16,256,256]{1,2,0:T(8,128)(2,1)}, u32[]{:S(2)}) copy-start(bf16[16,256,256]{1,2,0:T(8,128)(2,1)} %copy.9) | copy-start | bytes 6291460
Sparse Core Ops, SparseCore 0:
  9.6 19.4 all-gather.2
where the time goes:
time: 225 us; the launch traced here: 224 us
  local copies, waits for them, and re-layouts  52.8 us (23%)
  blocking collectives  42.6 us (19%)
  waiting for transfers between devices  41.8 us (19%)
  other arithmetic  38.8 us (17%)
  matrix products  19.3 us (9%)
  between operations  14.9 us (7%)
  starting transfers between devices  14.1 us (6%)
    gather x48, local copies, waits for them, and re-layouts  46.7 us
    psum x1, blocking collectives, local(): total_sq = lax.psum(jnp.sum(slopes * slopes), ('tile', 'pos'))  42.6 us
    all_gather x1, waiting for transfers between devices, local(): region_block = lax.all_gather(quarter, 'pos', axis=1, tiled=True)  21.1 us
    ppermute x4, waiting for transfers between devices, passed_along(): return lax.ppermute(x, axis, pairs)  20 us
    ppermute x4, starting transfers between devices, passed_along(): return lax.ppermute(x, axis, pairs)  14.1 us
    dot_general x4, matrix products, left_apply(): jnp.einsum('kn,pnm->pkm', table, stacked, preferred_element_type=jnp.floa...  10.4 us
    mul x1, other arithmetic, refine_block(): along_col = 0.5 * (window_f[:, :, 1:-1, 2:] - window_f[:, :, 1:-1, :-2])  9.2 us
    dot_general x4, matrix products, right_apply(): jnp.einsum('pkn,nm->pkm', stacked, table, preferred_element_type=jnp.floa...  8.89 us
  transfers between devices with their start and end apart: 5, of which 4 were waited for; matrix products, arithmetic and copies ran while one was open for 2% of the time, Pallas kernels for 0%

commit v1 on v0

v1 whole, which is shorter than its diff:
```python
import functools
import math

import jax
import jax.numpy as jnp
import numpy as np
from jax import lax
from jax.experimental import pallas as pl
from jax.experimental.pallas import tpu as pltpu
from jax.sharding import PartitionSpec as P

GC = 4
CHUNKS = 4
BATCH = 2
MESH_ID = pl.DeviceIdType.MESH


def dft_tables(length_n):
    indices = np.arange(length_n)
    products_mod = indices[:, None] * indices[None, :] % length_n
    angles = products_mod.astype(np.float32) * np.float32(2.0 * math.pi / length_n)
    factor = np.float32(1.0 / math.sqrt(length_n))
    cosine, sine = np.cos(angles) * factor, np.sin(angles) * factor
    forward = np.block([[cosine, sine], [-sine, cosine]])
    return jnp.asarray(forward, jnp.bfloat16), jnp.asarray(forward.T, jnp.bfloat16)


def halo_kernel(n_tile, margin, x_ref, pad_ref, send_sems, recv_sems, local_sem):
    t, p = lax.axis_index("tile"), lax.axis_index("pos")
    _, quarter, width = x_ref.shape
    rows = pad_ref.shape[1] - 2 * margin
    last = rows // quarter - 1
    c, r = t % GC, t // GC
    core, half = p % 2, p // 2
    near, far = p + 1 - 2 * core, p + 2 - 4 * half
    west, east = c > 0, c < GC - 1
    north, south = r > 0, r < n_tile // GC - 1
    yes = p >= 0
    is_first, is_last = p == 0, p == last
    tall, wide = rows + 2 * margin, width + 2 * margin

    def zero(cond, rows_at, cols_at):
        @pl.when(cond)
        def _():
            part = pad_ref.at[:, rows_at, cols_at]
            part[...] = jnp.zeros(part.shape, part.dtype)

    zero(jnp.logical_not(west), slice(0, tall), slice(0, margin))
    zero(jnp.logical_not(east), slice(0, tall), slice(margin + width, wide))
    zero(jnp.logical_not(north), slice(0, margin), slice(0, wide))
    zero(jnp.logical_not(south), slice(margin + rows, tall), slice(0, wide))

    barrier = pltpu.get_barrier_semaphore()
    is_end = jnp.logical_or(is_first, is_last)
    partners = [
        (yes, t, near),
        (yes, t, far),
        (west, t - 1, p),
        (east, t + 1, p),
        (jnp.logical_and(is_end, north), t - GC, p),
        (jnp.logical_and(is_end, south), t + GC, p),
    ]
    for cond, to_t, to_p in partners:
        @pl.when(cond)
        def _():
            pl.semaphore_signal(barrier, inc=1, device_id=(to_t, to_p), device_id_type=MESH_ID)
    ends = is_end.astype(jnp.int32)
    sides_met = west.astype(jnp.int32) + east.astype(jnp.int32)
    rows_met = north.astype(jnp.int32) + south.astype(jnp.int32)
    pl.semaphore_wait(barrier, 2 + sides_met + ends * rows_met)

    mine = pl.ds(pl.multiple_of(margin + p * quarter, quarter), quarter)
    its = pl.ds(pl.multiple_of(margin + far * quarter, quarter), quarter)
    nears = pl.ds(pl.multiple_of(margin + near * quarter, quarter), quarter)
    near_far = near + 2 - 4 * half
    nears_far = pl.ds(pl.multiple_of(margin + near_far * quarter, quarter), quarter)
    mid = slice(margin, margin + width)
    left, right = slice(0, margin), slice(margin + width, wide)
    every = slice(0, wide)
    sent = []

    def copy(index, src, dst, to_t, to_p):
        return pltpu.make_async_remote_copy(
            src_ref=src,
            dst_ref=dst,
            send_sem=send_sems.at[index],
            recv_sem=recv_sems.at[index],
            device_id=(to_t, to_p),
            device_id_type=MESH_ID,
        )

    def send(cond, index, src, dst, to_t, to_p):
        made = copy(index, src, dst, to_t, to_p)
        sent.append((cond, made))

        @pl.when(cond)
        def _():
            made.start()

    def receive(cond, index, dst):
        @pl.when(cond)
        def _():
            copy(index, dst, dst, t, near).wait_recv()

    def at(rows_at, cols_at):
        return pad_ref.at[:, rows_at, cols_at]

    own = pltpu.make_async_copy(x_ref, at(mine, mid), local_sem)
    own.start()
    send(east, 2, x_ref.at[:, :, width - margin : width], at(mine, left), t + 1, p)
    send(west, 3, x_ref.at[:, :, 0:margin], at(mine, right), t - 1, p)
    send(yes, 0, x_ref, at(mine, mid), t, far)
    send(yes, 1, x_ref, at(mine, mid), t, near)
    own.wait()
    receive(west, 2, at(mine, left))
    receive(east, 3, at(mine, right))
    piece = margin // CHUNKS
    base = 11
    for k in range(CHUNKS):
        up, down = slice(margin + rows + k * piece, margin + rows + (k + 1) * piece), slice(k * piece, (k + 1) * piece)
        top = slice(margin + k * piece, margin + (k + 1) * piece)
        bottom = slice(rows + k * piece, rows + (k + 1) * piece)
        send(jnp.logical_and(is_first, north), base + k, at(top, every), at(up, every), t - GC, p)
        send(jnp.logical_and(is_last, south), base + 3 * CHUNKS + k, at(bottom, every), at(down, every), t + GC, p)
    send(yes, 4, at(mine, left), at(mine, left), t, far)
    send(yes, 5, at(mine, right), at(mine, right), t, far)
    send(yes, 7, at(mine, left), at(mine, left), t, near)
    send(yes, 8, at(mine, right), at(mine, right), t, near)
    receive(yes, 0, at(its, mid))
    send(yes, 6, at(its, mid), at(its, mid), t, near)
    receive(yes, 4, at(its, left))
    send(yes, 9, at(its, left), at(its, left), t, near)
    receive(yes, 5, at(its, right))
    send(yes, 10, at(its, right), at(its, right), t, near)
    sides = [
        (base, south, margin + rows, is_first, core == 0),
        (base + 3 * CHUNKS, north, 0, is_last, core == 1),
    ]
    for start, inside, row, is_root, is_side in sides:
        for k in range(CHUNKS):
            part = at(slice(row + k * piece, row + (k + 1) * piece), every)
            root = jnp.logical_and(inside, is_root)
            holds = jnp.logical_and(inside, is_side)
            second = jnp.logical_and(holds, jnp.logical_not(is_root))
            receive(root, start + k, part)
            send(root, start + CHUNKS + k, part, part, t, far)
            receive(second, start + CHUNKS + k, part)
            send(holds, start + 2 * CHUNKS + k, part, part, t, near)
    receive(yes, 1, at(nears, mid))
    receive(yes, 7, at(nears, left))
    receive(yes, 8, at(nears, right))
    receive(yes, 6, at(nears_far, mid))
    receive(yes, 9, at(nears_far, left))
    receive(yes, 10, at(nears_far, right))
    for start, inside, row, is_root, is_side in sides:
        for k in range(CHUNKS):
            part = at(slice(row + k * piece, row + (k + 1) * piece), every)
            receive(jnp.logical_and(inside, jnp.logical_not(is_side)), start + 2 * CHUNKS + k, part)
    for cond, made in sent:
        @pl.when(cond)
        def _():
            made.wait_send()


def gather_halo(quarter, n_tile, n_pos, margin):
    if n_pos != 4 or quarter.shape[1] < margin:
        raise ValueError("unsupported split")
    rows = quarter.shape[1] * n_pos
    sems = 11 + 6 * CHUNKS
    return pl.pallas_call(
        functools.partial(halo_kernel, n_tile, margin),
        out_shape=jax.ShapeDtypeStruct((2, rows + 2 * margin, quarter.shape[2] + 2 * margin), quarter.dtype),
        in_specs=[pl.BlockSpec(memory_space=pltpu.VMEM)],
        out_specs=pl.BlockSpec(memory_space=pltpu.VMEM),
        scratch_shapes=[
            pltpu.SemaphoreType.DMA((sems,)),
            pltpu.SemaphoreType.DMA((sems,)),
            pltpu.SemaphoreType.DMA,
        ],
        compiler_params=pltpu.CompilerParams(collective_id=0, has_side_effects=True),
    )(quarter)


def fold(value):
    return jnp.sum(value.reshape(-1, 8, value.shape[-1]), axis=0)


def refine_kernel(
    batch, steps, off_ref, pad_ref, probe_ref, frames_ref, fwd_ref, bwd_ref, out_ref,
    planes, patch, slant, exits, halves, resid, inner, sums,
):
    step = pl.program_id(0)
    n = probe_ref.shape[1]
    tall, wide = pad_ref.shape[1], pad_ref.shape[2]
    lanes = 128
    blocks = n // lanes

    @pl.when(step == 0)
    def _():
        @pl.loop(0, tall // 32)
        def _(i):
            at = pl.ds(pl.multiple_of(i * 32, 32), 32)
            for part in range(2):
                value = pad_ref[part, at, :].astype(jnp.float32)
                slope = 0.5 * (pltpu.roll(value, wide - 1, 1) - pltpu.roll(value, 1, 1))
                for k in range(wide // lanes):
                    cols = slice(k * lanes, (k + 1) * lanes)
                    planes[part, k, at, :] = value[:, cols]
                    planes[2 + part, k, at, :] = slope[:, cols]

    column = lax.broadcasted_iota(jnp.int32, (8, lanes), 1)

    for b in range(batch):
        j = step * batch + b
        row, col = off_ref[0, j], off_ref[1, j]
        block, shift = col // lanes, col % lanes
        turn = (lanes - shift) % lanes
        for part in range(4):
            high = n + 8 if part < 2 else n
            first = row - 1 if part < 2 else row
            target = patch.at[b, part] if part < 2 else slant.at[b, part - 2]
            keep = lax.broadcasted_iota(jnp.int32, (high, lanes), 1) < lanes - shift
            turned = [
                pltpu.roll(planes[part, block + k, pl.ds(first, high), :], turn, 1) for k in range(blocks + 1)
            ]
            for k in range(blocks):
                target[:, k * lanes : (k + 1) * lanes] = jnp.where(keep, turned[k], turned[k + 1])
        o_re, o_im = patch[b, 0, 1 : n + 1, :], patch[b, 1, 1 : n + 1, :]
        p_re, p_im = probe_ref[0], probe_ref[1]
        exits[b, :n, :] = (p_re * o_re - p_im * o_im).astype(jnp.bfloat16)
        exits[b, n:, :] = (p_re * o_im + p_im * o_re).astype(jnp.bfloat16)
    for b in range(batch):
        half = jnp.dot(fwd_ref[...], exits[b], preferred_element_type=jnp.float32)
        halves[b * n : (b + 1) * n, :n] = half[:n].astype(jnp.bfloat16)
        halves[b * n : (b + 1) * n, n:] = half[n:].astype(jnp.bfloat16)
    losses = []
    for b in range(batch):
        wave = jnp.dot(halves[b * n : (b + 1) * n, :], bwd_ref[...], preferred_element_type=jnp.float32)
        f_re, f_im = wave[:, :n], wave[:, n:]
        square = f_re * f_re + f_im * f_im
        keep_part = 1.0 - frames_ref[b].astype(jnp.float32) * lax.rsqrt(jnp.maximum(square, 0.0625))
        losses.append(fold(square * (keep_part * keep_part)))
        resid[b, :n, :] = (f_re * keep_part).astype(jnp.bfloat16)
        resid[b, n:, :] = (f_im * keep_part).astype(jnp.bfloat16)
    for b in range(batch):
        back = jnp.dot(bwd_ref[...], resid[b], preferred_element_type=jnp.float32)
        inner[b * n : (b + 1) * n, :n] = back[:n].astype(jnp.bfloat16)
        inner[b * n : (b + 1) * n, n:] = back[n:].astype(jnp.bfloat16)
    for b in range(batch):
        j = step * batch + b
        wave = jnp.dot(inner[b * n : (b + 1) * n, :], fwd_ref[...], preferred_element_type=jnp.float32)
        g_re, g_im = wave[:, :n], wave[:, n:]
        p_re, p_im = probe_ref[0], probe_ref[1]
        q_re = g_re * p_re + g_im * p_im
        q_im = g_re * p_im - g_im * p_re
        d_re = patch[b, 0, 2 : n + 2, :] - patch[b, 0, 0:n, :]
        d_im = patch[b, 1, 2 : n + 2, :] - patch[b, 1, 0:n, :]
        by_row = fold(q_re * d_re - q_im * d_im) * 0.5
        by_col = fold(q_re * slant[b, 0] - q_im * slant[b, 1])
        for which, value in enumerate((by_row, by_col, losses[b] * (1.0 / (n * n)))):
            line = jnp.sum(value, axis=0, keepdims=True)
            short = line[:, :lanes]
            for k in range(1, blocks):
                short = short + line[:, k * lanes : (k + 1) * lanes]
            sums[which, pl.ds(j, 1), :] = short

    @pl.when(step == steps - 1)
    def _():
        count = sums.shape[1]
        diagonal = lax.broadcasted_iota(jnp.int32, (count, lanes), 0) == lax.broadcasted_iota(jnp.int32, (count, lanes), 1)
        lines = []
        for which in range(3):
            full = jnp.sum(sums[which], axis=1, keepdims=True)
            lines.append(jnp.sum(jnp.where(diagonal, full, 0.0), axis=0, keepdims=True))
        squares = jnp.sum(lines[0] * lines[0] + lines[1] * lines[1], axis=1, keepdims=True)
        lines.append(jnp.broadcast_to(squares, (1, lanes)))
        out_ref[...] = jnp.concatenate(lines + [jnp.zeros((4, lanes), jnp.float32)], axis=0)


def refine(padded, probe, frames, offsets):
    count, n, _ = frames.shape
    if count % BATCH or count > 128 or n % 128:
        raise ValueError("unsupported sizes")
    forward, backward = dft_tables(n)
    tall, wide = padded.shape[1:]
    steps = count // BATCH
    vmem = lambda shape, kind: pltpu.VMEM(shape, kind)
    whole = lambda shape: pl.BlockSpec(shape, lambda i: (0,) * len(shape))
    return pl.pallas_call(
        functools.partial(refine_kernel, BATCH, steps),
        grid=(steps,),
        out_shape=jax.ShapeDtypeStruct((8, 128), jnp.float32),
        in_specs=[
            pl.BlockSpec(memory_space=pltpu.SMEM),
            whole(padded.shape),
            whole(probe.shape),
            pl.BlockSpec((BATCH, n, n), lambda i: (i, 0, 0)),
            whole(forward.shape),
            whole(backward.shape),
        ],
        out_specs=whole((8, 128)),
        scratch_shapes=[
            vmem((4, wide // 128, tall + 8, 128), jnp.float32),
            vmem((BATCH, 2, n + 8, n), jnp.float32),
            vmem((BATCH, 2, n, n), jnp.float32),
            vmem((BATCH, 2 * n, n), jnp.bfloat16),
            vmem((BATCH * n, 2 * n), jnp.bfloat16),
            vmem((BATCH, 2 * n, n), jnp.bfloat16),
            vmem((BATCH * n, 2 * n), jnp.bfloat16),
            vmem((3, count, 128), jnp.float32),
        ],
        compiler_params=pltpu.CompilerParams(vmem_limit_bytes=56 * 1024 * 1024),
    )(offsets, padded, probe, frames, forward, backward)


def scale_kernel(n_tile, n_pos, positions, mine_ref, shifts_ref, losses_ref, others, send_sems, recv_sems):
    devices = n_tile * n_pos
    me = lax.axis_index("tile") * n_pos + lax.axis_index("pos")
    count = shifts_ref.shape[1]

    def to(k):
        other = (me + k) % devices
        return (other // n_pos, other % n_pos)

    barrier = pltpu.get_barrier_semaphore()

    def greet(k, carry):
        pl.semaphore_signal(barrier, inc=1, device_id=to(k), device_id_type=MESH_ID)
        return carry

    lax.fori_loop(1, devices, greet, 0)
    pl.semaphore_wait(barrier, devices - 1)

    def copy(k):
        return pltpu.make_async_remote_copy(
            src_ref=mine_ref,
            dst_ref=others.at[k - 1],
            send_sem=send_sems.at[k - 1],
            recv_sem=recv_sems.at[k - 1],
            device_id=to(k),
            device_id_type=MESH_ID,
        )

    def begin(k, carry):
        copy(k).start()
        return carry

    def finish(k, carry):
        copy(k).wait()
        return carry

    lax.fori_loop(1, devices, begin, 0)
    lax.fori_loop(1, devices, finish, 0)
    total = jnp.sum(others[...], axis=0) + mine_ref[...]
    scale = jnp.sqrt(total[3:4, :] * (1.0 / positions) + 1e-06)
    shifts_ref[...] = (-mine_ref[0:2, :] / scale)[:, :count]
    losses_ref[...] = mine_ref[2:3, :count]


def normalise(lines, count, n_tile, n_pos):
    devices = n_tile * n_pos
    whole = pl.BlockSpec(memory_space=pltpu.VMEM)
    return pl.pallas_call(
        functools.partial(scale_kernel, n_tile, n_pos, count * devices),
        out_shape=(jax.ShapeDtypeStruct((2, count), jnp.float32), jax.ShapeDtypeStruct((1, count), jnp.float32)),
        in_specs=[whole],
        out_specs=(whole, whole),
        scratch_shapes=[
            pltpu.VMEM((devices - 1, 8, 128), jnp.float32),
            pltpu.SemaphoreType.DMA((devices - 1,)),
            pltpu.SemaphoreType.DMA((devices - 1,)),
        ],
        compiler_params=pltpu.CompilerParams(collective_id=1, has_side_effects=True),
    )(lines)


def solution(mesh):
    n_tile, n_pos = mesh.shape["tile"], mesh.shape["pos"]

    def local(object_tiles, probe, frames, offsets):
        padded = gather_halo(object_tiles[0], n_tile, n_pos, probe.shape[1] // 2)
        lines = refine(padded, probe, frames, offsets)
        shifts, losses = normalise(lines, frames.shape[0], n_tile, n_pos)
        return shifts, losses[0]

    in_specs = (
        P("tile", None, "pos", None),
        P(),
        P(("tile", "pos"), None, None),
        P(None, ("tile", "pos")),
    )
    out_specs = (P(None, ("tile", "pos")), P(("tile", "pos")))
    return jax.shard_map(local, mesh=mesh, in_specs=in_specs, out_specs=out_specs, check_vma=False)
```

time: 225 us -> 63.1 us (0.28)
  Pallas kernels: 0 us -> 59.9 us
  local copies, waits for them, and re-layouts: 52.8 us -> 2.36 us
  blocking collectives: 42.6 us -> 0 us
  waiting for transfers between devices: 41.8 us -> 0 us
  other arithmetic: 38.8 us -> 0 us
  matrix products: 19.3 us -> 0 us
  between operations: 14.9 us -> 0.65 us
  starting transfers between devices: 14.1 us -> 0 us
    pallas_call x0 -> x3, Pallas kernels: none -> 59.9 us  [the longest x1 24.6 us: gather_halo(): pl.pallas_call(functools.partial(halo_kernel, n_tile, margin), out_shape=...]
    gather x48 -> x0, local copies, waits for them, and re-layouts: 46.7 us -> none
    psum x1 -> x0, blocking collectives: 42.6 us -> none  [local(): total_sq = lax.psum(jnp.sum(slopes * slopes), ('tile', 'pos'))]
    all_gather x1 -> x0, waiting for transfers between devices: 21.1 us -> none  [local(): region_block = lax.all_gather(quarter, 'pos', axis=1, tiled=True)]
    ppermute x4 -> x0, waiting for transfers between devices: 20 us -> none  [passed_along(): return lax.ppermute(x, axis, pairs)]
    dot_general x8 -> x0, matrix products: 19.3 us -> none  [the longest x4 10.4 us: left_apply(): jnp.einsum('kn,pnm->pkm', table, stacked, preferred_element_type=jnp.floa...]
    ppermute x4 -> x0, starting transfers between devices: 14.1 us -> none  [passed_along(): return lax.ppermute(x, axis, pairs)]
    reduce_sum x3 -> x0, other arithmetic: 12.6 us -> none  [the longest x1 8.2 us: slope_of(): return jnp.sum(wave_re * probed_re + wave_im * probed_im, axis=(1, 2))]
  transfers between devices with their start and end apart: 5 -> 0, of which waited for: 4 -> 0; matrix products, arithmetic and copies ran while one was open for 2% -> 0% of each run, Pallas kernels for 0% -> 0%
where the time goes in v1:
time: 63.1 us; the launch traced here: 62.9 us
  Pallas kernels  59.9 us (95%)
  local copies, waits for them, and re-layouts  2.36 us (4%)
  between operations  0.65 us (1%)
    pallas_call x1, Pallas kernels, gather_halo(): pl.pallas_call(functools.partial(halo_kernel, n_tile, margin), out_shape=...  24.6 us
    pallas_call x1, Pallas kernels, refine(): pl.pallas_call(functools.partial(refine_kernel, BATCH, steps), grid=(step...  23.7 us
    pallas_call x1, Pallas kernels, normalise(): pl.pallas_call(functools.partial(scale_kernel, n_tile, n_pos, count * dev...  11.6 us
    unnamed x2, local copies, waits for them, and re-layouts  2.36 us

profile of v1, /device:TPU:0, one launch (start us, length us, event | category | flops | bytes accessed | tf_op | source)
XLA Modules:
  0.0 62.9 jit_solution(16141126600350462708)
XLA Ops:
  0.6 24.6 %shard_map.77.pad_ref = bf16[2,768,768]{2,1,0:T(8,128)(2,1)} custom-call(bf16[2,128,512]{2,1,0:T(8,128)(2,1)} %bitcast.2), custom_call_target="tpu_custom_call" | custom-call | tf_op jit(solution)/shard_map/pallas_call | solution.py:170
  25.2 23.7 %shard_map.78.mine_ref = f32[8,128]{1,0:T(8,128)} custom-call(s32[2,16]{1,0:T(2,128)} %off_ref.1, bf16[2,768,768]{2,1,0:T(8,128)(2,1)} %shard_map.77.pad_ref, f32[2,256,256]{2,1,0:T(8,128)} %probe_ref.1, bf16[16,256,256]{2,1,0:T(8,128)(2,1)} %frames_ref.1, bf16[512,512]{1,0:T(8,128)(2,1)} %constant.4.clone.fwd_ref, bf16[512,512]{1,0:T(8,128)(2,1)} %constant.5.clone.bwd_ref), custom_call_target="tpu_custom_call" | custom-call | tf_op jit(solution)/shard_map/pallas_call | solution.py:289
  48.9 11.6 %shard_map.79 = (f32[2,16]{1,0:T(2,128)}, f32[1,16]{1,0:T(1,128)}) custom-call(f32[8,128]{1,0:T(8,128)} %shard_map.78.mine_ref), custom_call_target="tpu_custom_call" | custom-call | tf_op jit(solution)/shard_map/pallas_call | solution.py:363
  60.6 1.2 %copy.10 = f32[2,16]{1,0:T(2,128)} copy(f32[2,16]{1,0:T(2,128)} %get-tuple-element.8) | data formatting | bytes 256
  61.8 1.1 %copy.11 = f32[16]{0:T(128)} copy(f32[16]{0:T(128)} %bitcast.3) | data formatting | bytes 128

commit v2 on v1

--- a/solution.py
+++ b/solution.py
@@ -25,7 +25,14 @@
     return jnp.asarray(forward, jnp.bfloat16), jnp.asarray(forward.T, jnp.bfloat16)
 
 
-def halo_kernel(n_tile, margin, x_ref, pad_ref, send_sems, recv_sems, local_sem):
+def peer(axis, k, n_tile, n_pos):
+    t, p = lax.axis_index("tile"), lax.axis_index("pos")
+    if axis == "pos":
+        return (t, lax.rem(p + k, n_pos))
+    return (lax.rem(t + k, n_tile), p)
+
+
+def gather_halo(n_tile, n_pos, margin, x_ref, pad_ref, send_sems, recv_sems, local_sem, convert):
     t, p = lax.axis_index("tile"), lax.axis_index("pos")
     _, quarter, width = x_ref.shape
     rows = pad_ref.shape[1] - 2 * margin
@@ -51,23 +58,10 @@
     zero(jnp.logical_not(south), slice(margin + rows, tall), slice(0, wide))
 
     barrier = pltpu.get_barrier_semaphore()
-    is_end = jnp.logical_or(is_first, is_last)
-    partners = [
-        (yes, t, near),
-        (yes, t, far),
-        (west, t - 1, p),
-        (east, t + 1, p),
-        (jnp.logical_and(is_end, north), t - GC, p),
-        (jnp.logical_and(is_end, south), t + GC, p),
-    ]
-    for cond, to_t, to_p in partners:
-        @pl.when(cond)
-        def _():
-            pl.semaphore_signal(barrier, inc=1, device_id=(to_t, to_p), device_id_type=MESH_ID)
-    ends = is_end.astype(jnp.int32)
-    sides_met = west.astype(jnp.int32) + east.astype(jnp.int32)
-    rows_met = north.astype(jnp.int32) + south.astype(jnp.int32)
-    pl.semaphore_wait(barrier, 2 + sides_met + ends * rows_met)
+    for axis, devices in (("pos", n_pos), ("tile", n_tile)):
+        for k in range(1, devices):
+            pl.semaphore_signal(barrier, inc=1, device_id=peer(axis, k, n_tile, n_pos), device_id_type=MESH_ID)
+    pl.semaphore_wait(barrier, n_pos + n_tile - 2)
 
     mine = pl.ds(pl.multiple_of(margin + p * quarter, quarter), quarter)
     its = pl.ds(pl.multiple_of(margin + far * quarter, quarter), quarter)
@@ -152,33 +146,36 @@
     receive(yes, 6, at(nears_far, mid))
     receive(yes, 9, at(nears_far, left))
     receive(yes, 10, at(nears_far, right))
+    convert(margin, margin + rows)
     for start, inside, row, is_root, is_side in sides:
         for k in range(CHUNKS):
             part = at(slice(row + k * piece, row + (k + 1) * piece), every)
             receive(jnp.logical_and(inside, jnp.logical_not(is_side)), start + 2 * CHUNKS + k, part)
+    convert(0, margin)
+    convert(margin + rows, tall)
     for cond, made in sent:
         @pl.when(cond)
         def _():
             made.wait_send()
 
 
-def gather_halo(quarter, n_tile, n_pos, margin):
-    if n_pos != 4 or quarter.shape[1] < margin:
-        raise ValueError("unsupported split")
-    rows = quarter.shape[1] * n_pos
-    sems = 11 + 6 * CHUNKS
-    return pl.pallas_call(
-        functools.partial(halo_kernel, n_tile, margin),
-        out_shape=jax.ShapeDtypeStruct((2, rows + 2 * margin, quarter.shape[2] + 2 * margin), quarter.dtype),
-        in_specs=[pl.BlockSpec(memory_space=pltpu.VMEM)],
-        out_specs=pl.BlockSpec(memory_space=pltpu.VMEM),
-        scratch_shapes=[
-            pltpu.SemaphoreType.DMA((sems,)),
-            pltpu.SemaphoreType.DMA((sems,)),
-            pltpu.SemaphoreType.DMA,
-        ],
-        compiler_params=pltpu.CompilerParams(collective_id=0, has_side_effects=True),
-    )(quarter)
+def shared_sum(axis, devices, n_tile, n_pos, mine_ref, others, send_sems, recv_sems):
+    copies = [
+        pltpu.make_async_remote_copy(
+            src_ref=mine_ref,
+            dst_ref=others.at[k - 1],
+            send_sem=send_sems.at[k - 1],
+            recv_sem=recv_sems.at[k - 1],
+            device_id=peer(axis, k, n_tile, n_pos),
+            device_id_type=MESH_ID,
+        )
+        for k in range(1, devices)
+    ]
+    for made in copies:
+        made.start()
+    for made in copies:
+        made.wait()
+    return jnp.sum(others[...], axis=0) + mine_ref[...]
 
 
 def fold(value):
@@ -186,8 +183,10 @@
 
 
 def refine_kernel(
-    batch, steps, off_ref, pad_ref, probe_ref, frames_ref, fwd_ref, bwd_ref, out_ref,
-    planes, patch, slant, exits, halves, resid, inner, sums,
+    batch, steps, n_tile, n_pos, off_ref, x_ref, probe_hbm, frames_ref, fwd_hbm, bwd_hbm, out_ref,
+    pad_ref, probe_ref, fwd_ref, bwd_ref, planes, patch, slant, exits, halves, resid, inner, sums,
+    send_sems, recv_sems, local_sems, pos_line, tile_line, pos_others, tile_others,
+    pos_sends, pos_recvs, tile_sends, tile_recvs,
 ):
     step = pl.program_id(0)
     n = probe_ref.shape[1]
@@ -195,20 +194,30 @@
     lanes = 128
     blocks = n // lanes
 
-    @pl.when(step == 0)
-    def _():
-        @pl.loop(0, tall // 32)
+    def convert(first, last):
+        @pl.loop(first // 32, last // 32)
         def _(i):
             at = pl.ds(pl.multiple_of(i * 32, 32), 32)
+            lower = pl.ds(pl.multiple_of(i * 32 + 8, 8), 32)
             for part in range(2):
                 value = pad_ref[part, at, :].astype(jnp.float32)
                 slope = 0.5 * (pltpu.roll(value, wide - 1, 1) - pltpu.roll(value, 1, 1))
                 for k in range(wide // lanes):
                     cols = slice(k * lanes, (k + 1) * lanes)
-                    planes[part, k, at, :] = value[:, cols]
-                    planes[2 + part, k, at, :] = slope[:, cols]
-
-    column = lax.broadcasted_iota(jnp.int32, (8, lanes), 1)
+                    planes[part, k, lower, :] = value[:, cols]
+                    planes[2 + part, k, lower, :] = slope[:, cols]
+
+    @pl.when(step == 0)
+    def _():
+        loads = [
+            pltpu.make_async_copy(source, target, local_sems.at[k])
+            for k, (source, target) in enumerate(((probe_hbm, probe_ref), (fwd_hbm, fwd_ref), (bwd_hbm, bwd_ref)))
+        ]
+        for load in loads:
+            load.start()
+        gather_halo(n_tile, n_pos, n // 2, x_ref, pad_ref, send_sems, recv_sems, local_sems.at[3], convert)
+        for load in loads:
+            load.wait()
 
     for b in range(batch):
         j = step * batch + b
@@ -217,7 +226,7 @@
         turn = (lanes - shift) % lanes
         for part in range(4):
             high = n + 8 if part < 2 else n
-            first = row - 1 if part < 2 else row
+            first = row + 7 if part < 2 else row + 8
             target = patch.at[b, part] if part < 2 else slant.at[b, part - 2]
             keep = lax.broadcasted_iota(jnp.int32, (high, lanes), 1) < lanes - shift
             turned = [
@@ -273,34 +282,43 @@
             full = jnp.sum(sums[which], axis=1, keepdims=True)
             lines.append(jnp.sum(jnp.where(diagonal, full, 0.0), axis=0, keepdims=True))
         squares = jnp.sum(lines[0] * lines[0] + lines[1] * lines[1], axis=1, keepdims=True)
-        lines.append(jnp.broadcast_to(squares, (1, lanes)))
+        pos_line[...] = jnp.broadcast_to(squares, (1, lanes))
+        tile_line[...] = shared_sum("pos", n_pos, n_tile, n_pos, pos_line, pos_others, pos_sends, pos_recvs)
+        lines.append(shared_sum("tile", n_tile, n_tile, n_pos, tile_line, tile_others, tile_sends, tile_recvs))
         out_ref[...] = jnp.concatenate(lines + [jnp.zeros((4, lanes), jnp.float32)], axis=0)
 
 
-def refine(padded, probe, frames, offsets):
+def refine(quarter, probe, frames, offsets, n_tile, n_pos):
     count, n, _ = frames.shape
-    if count % BATCH or count > 128 or n % 128:
+    _, height, width = quarter.shape
+    if count % BATCH or count > 128 or n % 128 or n_pos != 4 or height < n // 2:
         raise ValueError("unsupported sizes")
     forward, backward = dft_tables(n)
-    tall, wide = padded.shape[1:]
+    tall, wide = height * n_pos + n, width + n
     steps = count // BATCH
-    vmem = lambda shape, kind: pltpu.VMEM(shape, kind)
+    sems = 11 + 6 * CHUNKS
+    vmem, dma = pltpu.VMEM, pltpu.SemaphoreType.DMA
     whole = lambda shape: pl.BlockSpec(shape, lambda i: (0,) * len(shape))
+    anywhere = pl.BlockSpec(memory_space=pl.ANY)
     return pl.pallas_call(
-        functools.partial(refine_kernel, BATCH, steps),
+        functools.partial(refine_kernel, BATCH, steps, n_tile, n_pos),
         grid=(steps,),
         out_shape=jax.ShapeDtypeStruct((8, 128), jnp.float32),
         in_specs=[
             pl.BlockSpec(memory_space=pltpu.SMEM),
-            whole(padded.shape),
-            whole(probe.shape),
+            whole(quarter.shape),
+            anywhere,
             pl.BlockSpec((BATCH, n, n), lambda i: (i, 0, 0)),
-            whole(forward.shape),
-            whole(backward.shape),
+            anywhere,
+            anywhere,
         ],
         out_specs=whole((8, 128)),
         scratch_shapes=[
-            vmem((4, wide // 128, tall + 8, 128), jnp.float32),
+            vmem((2, tall, wide), jnp.bfloat16),
+            vmem(probe.shape, jnp.float32),
+            vmem(forward.shape, jnp.bfloat16),
+            vmem(backward.shape, jnp.bfloat16),
+            vmem((4, wide // 128, tall + 16, 128), jnp.float32),
             vmem((BATCH, 2, n + 8, n), jnp.float32),
             vmem((BATCH, 2, n, n), jnp.float32),
             vmem((BATCH, 2 * n, n), jnp.bfloat16),
@@ -308,69 +326,38 @@
             vmem((BATCH, 2 * n, n), jnp.bfloat16),
             vmem((BATCH * n, 2 * n), jnp.bfloat16),
             vmem((3, count, 128), jnp.float32),
+            dma((sems,)),
+            dma((sems,)),
+            dma((4,)),
+            vmem((1, 128), jnp.float32),
+            vmem((1, 128), jnp.float32),
+            vmem((n_pos - 1, 1, 128), jnp.float32),
+            vmem((n_tile - 1, 1, 128), jnp.float32),
+            dma((n_pos - 1,)),
+            dma((n_pos - 1,)),
+            dma((n_tile - 1,)),
+            dma((n_tile - 1,)),
         ],
-        compiler_params=pltpu.CompilerParams(vmem_limit_bytes=56 * 1024 * 1024),
-    )(offsets, padded, probe, frames, forward, backward)
-
-
-def scale_kernel(n_tile, n_pos, positions, mine_ref, shifts_ref, losses_ref, others, send_sems, recv_sems):
-    devices = n_tile * n_pos
-    me = lax.axis_index("tile") * n_pos + lax.axis_index("pos")
+        compiler_params=pltpu.CompilerParams(
+            vmem_limit_bytes=56 * 1024 * 1024, collective_id=0, has_side_effects=True
+        ),
+    )(offsets, quarter, probe, frames, forward, backward)
+
+
+def scale_kernel(positions, lines_ref, shifts_ref, losses_ref):
     count = shifts_ref.shape[1]
-
-    def to(k):
-        other = (me + k) % devices
-        return (other // n_pos, other % n_pos)
-
-    barrier = pltpu.get_barrier_semaphore()
-
-    def greet(k, carry):
-        pl.semaphore_signal(barrier, inc=1, device_id=to(k), device_id_type=MESH_ID)
-        return carry
-
-    lax.fori_loop(1, devices, greet, 0)
-    pl.semaphore_wait(barrier, devices - 1)
-
-    def copy(k):
-        return pltpu.make_async_remote_copy(
-            src_ref=mine_ref,
-            dst_ref=others.at[k - 1],
-            send_sem=send_sems.at[k - 1],
-            recv_sem=recv_sems.at[k - 1],
-            device_id=to(k),
-            device_id_type=MESH_ID,
-        )
-
-    def begin(k, carry):
-        copy(k).start()
-        return carry
-
-    def finish(k, carry):
-        copy(k).wait()
-        return carry
-
-    lax.fori_loop(1, devices, begin, 0)
-    lax.fori_loop(1, devices, finish, 0)
-    total = jnp.sum(others[...], axis=0) + mine_ref[...]
-    scale = jnp.sqrt(total[3:4, :] * (1.0 / positions) + 1e-06)
-    shifts_ref[...] = (-mine_ref[0:2, :] / scale)[:, :count]
-    losses_ref[...] = mine_ref[2:3, :count]
-
-
-def normalise(lines, count, n_tile, n_pos):
-    devices = n_tile * n_pos
-    whole = pl.BlockSpec(memory_space=pltpu.VMEM)
+    scale = jnp.sqrt(lines_ref[3:4, :] * (1.0 / positions) + 1e-06)
+    shifts_ref[...] = (-lines_ref[0:2, :] / scale)[:, :count]
+    losses_ref[...] = lines_ref[2:3, :count]
+
+
+def normalise(lines, count, positions):
+    block = pl.BlockSpec(memory_space=pltpu.VMEM)
     return pl.pallas_call(
-        functools.partial(scale_kernel, n_tile, n_pos, count * devices),
+        functools.partial(scale_kernel, positions),
         out_shape=(jax.ShapeDtypeStruct((2, count), jnp.float32), jax.ShapeDtypeStruct((1, count), jnp.float32)),
-        in_specs=[whole],
-        out_specs=(whole, whole),
-        scratch_shapes=[
-            pltpu.VMEM((devices - 1, 8, 128), jnp.float32),
-            pltpu.SemaphoreType.DMA((devices - 1,)),
-            pltpu.SemaphoreType.DMA((devices - 1,)),
-        ],
-        compiler_params=pltpu.CompilerParams(collective_id=1, has_side_effects=True),
+        in_specs=[block],
+        out_specs=(block, block),
     )(lines)
 
 
@@ -378,9 +365,9 @@
     n_tile, n_pos = mesh.shape["tile"], mesh.shape["pos"]
 
     def local(object_tiles, probe, frames, offsets):
-        padded = gather_halo(object_tiles[0], n_tile, n_pos, probe.shape[1] // 2)
-        lines = refine(padded, probe, frames, offsets)
-        shifts, losses = normalise(lines, frames.shape[0], n_tile, n_pos)
+        count = frames.shape[0]
+        lines = refine(object_tiles[0], probe, frames, offsets, n_tile, n_pos)
+        shifts, losses = normalise(lines, count, count * n_tile * n_pos)
         return shifts, losses[0]
 
     in_specs = (

time: 63.1 us -> 54.4 us (0.86)
  Pallas kernels: 59.9 us -> 53.4 us
  local copies, waits for them, and re-layouts: 2.36 us -> 0 us
    pallas_call x3 -> x2, Pallas kernels: 59.9 us -> 53.4 us  [the longest x1 52.2 us: refine(): pl.pallas_call(functools.partial(refine_kernel, BATCH, steps, n_tile, n_p...]
    unnamed x2 -> x0, local copies, waits for them, and re-layouts: 2.36 us -> none
where the time goes in v2:
time: 54.4 us; the launch traced here: 54.1 us
  Pallas kernels  53.4 us (98%)
  between operations  0.64 us (1%)
    pallas_call x1, Pallas kernels, refine(): pl.pallas_call(functools.partial(refine_kernel, BATCH, steps, n_tile, n_p...  52.2 us
    pallas_call x1, Pallas kernels, normalise(): pl.pallas_call(functools.partial(scale_kernel, positions), out_shape=(jax...  1.25 us

profile of v2, /device:TPU:0, one launch (start us, length us, event | category | flops | bytes accessed | tf_op | source)
XLA Modules:
  0.0 54.1 jit_solution(12795673760987200416)
XLA Ops:
  0.6 52.2 %shard_map.77.lines_ref = f32[8,128]{1,0:T(8,128)} custom-call(s32[2,16]{1,0:T(2,128)} %off_ref.1, bf16[2,128,512]{2,1,0:T(8,128)(2,1)} %bitcast.2, f32[2,256,256]{2,1,0:T(8,128)} %probe_hbm.1, bf16[16,256,256]{2,1,0:T(8,128)(2,1)} %frames_ref.1, bf16[512,512]{1,0:T(8,128)(2,1)} %constant.4.clone.fwd_hbm, bf16[512,512]{1,0:T(8,128)(2,1)} %constant.5.clone.bwd_hbm), custom_call_target="tpu_custom_call" | custom-call | tf_op jit(solution)/shard_map/pallas_call | solution.py:303
  52.8 1.3 %shard_map.78 = (f32[2,16]{1,0:T(2,128)}, f32[1,16]{1,0:T(1,128)}) custom-call(f32[8,128]{1,0:T(8,128)} %shard_map.77.lines_ref), custom_call_target="tpu_custom_call" | custom-call | tf_op jit(solution)/shard_map/pallas_call | solution.py:356

commit v3 on v2

--- a/solution.py
+++ b/solution.py
@@ -11,7 +11,7 @@
 
 GC = 4
 CHUNKS = 4
-BATCH = 2
+BATCH = 4
 MESH_ID = pl.DeviceIdType.MESH
 
 

time: 54.4 us -> 51.7 us (0.950)
  Pallas kernels: 53.4 us -> 50.9 us
    pallas_call x1, Pallas kernels: 52.2 us -> 49.6 us  [refine(): pl.pallas_call(functools.partial(refine_kernel, BATCH, steps, n_tile, n_p...]
where the time goes in v3:
time: 51.7 us; the launch traced here: 51.5 us
  Pallas kernels  50.9 us (98%)
  between operations  0.64 us (1%)
    pallas_call x1, Pallas kernels, refine(): pl.pallas_call(functools.partial(refine_kernel, BATCH, steps, n_tile, n_p...  49.6 us
    pallas_call x1, Pallas kernels, normalise(): pl.pallas_call(functools.partial(scale_kernel, positions), out_shape=(jax...  1.25 us

profile of v3, /device:TPU:0, one launch (start us, length us, event | category | flops | bytes accessed | tf_op | source)
XLA Modules:
  0.0 51.5 jit_solution(14455553633996187006)
XLA Ops:
  0.6 49.6 %shard_map.77.lines_ref = f32[8,128]{1,0:T(8,128)} custom-call(s32[2,16]{1,0:T(2,128)} %off_ref.1, bf16[2,128,512]{2,1,0:T(8,128)(2,1)} %bitcast.2, f32[2,256,256]{2,1,0:T(8,128)} %probe_hbm.1, bf16[16,256,256]{2,1,0:T(8,128)(2,1)} %frames_ref.1, bf16[512,512]{1,0:T(8,128)(2,1)} %constant.4.clone.fwd_hbm, bf16[512,512]{1,0:T(8,128)(2,1)} %constant.5.clone.bwd_hbm), custom_call_target="tpu_custom_call" | custom-call | tf_op jit(solution)/shard_map/pallas_call | solution.py:303
  50.2 1.3 %shard_map.78 = (f32[2,16]{1,0:T(2,128)}, f32[1,16]{1,0:T(1,128)}) custom-call(f32[8,128]{1,0:T(8,128)} %shard_map.77.lines_ref), custom_call_target="tpu_custom_call" | custom-call | tf_op jit(solution)/shard_map/pallas_call | solution.py:356
